TPU v7x, 256 devices: a whole 4x4x8 slice. The times are simulated.
256 devices in a mesh: row: 8 (over z), col: 8 (over y, core), depth: 4 (over x).
Axes of the slice: x: 4, y: 4, z: 8, core: 2. Of those that a mesh axis runs over, the one named last changes fastest.
Arguments:
- a21_leaf: float32 [4, 4096, 2048], P('depth', 'row', 'col'), may hold values from -1.2 to 1.2
- a12_leaf: float32 [4, 2048, 4096], P('depth', 'row', 'col'), may hold values from -1.2 to 1.2
- uinv_leaf: float32 [4, 2048, 2048], P('depth', None, 'col'), may hold values from -0.2 to 1.5, as said below
- linv_leaf: float32 [4, 2048, 2048], P('depth', 'row'), may hold values from -0.2 to 1.5, as said below
- live: int32 [4], P('depth'), may hold values from 16 to 32
- row_map: int32 [4, 32], P('depth', 'row'), may hold values from 0 to 63, as said below
- col_map: int32 [4, 32], P('depth', 'col'), may hold values from 0 to 63, as said below
- a22_anc: float32 [8192, 8192], P(('row', 'depth'), 'col'), may hold values from -6 to 6
- a21_anc: float32 [8192, 2048], P(('row', 'depth'), 'col'), may hold values from -1.2 to 1.2
- a12_anc: float32 [2048, 8192], P(('row', 'depth'), 'col'), may hold values from -1.2 to 1.2
- uinv_anc: float32 [2048, 2048], P(None, 'col'), may hold values from -0.2 to 1.5, as said below
- linv_anc: float32 [2048, 2048], P(('row', 'depth')), may hold values from -0.2 to 1.5, as said below
Outputs:
- leaf_lower: float32 [4, 4096, 2048], P('depth', 'row', 'col')
- leaf_upper: float32 [4, 2048, 4096], P('depth', 'row', 'col')
- anc_lower: float32 [8192, 2048], P(('row', 'depth'), 'col')
- anc_upper: float32 [2048, 8192], P(('row', 'depth'), 'col')
- anc_schur: float32 [8192, 8192], P(('row', 'depth'), 'col')
Inputs may be any that keep to these rules, and one draw needn't show every extreme that they name: `uinv_leaf`: upper triangular: zero below the diagonal, diagonal between 0.5 and 1.5. `linv_leaf`: lower triangular: zero above the diagonal, diagonal between 0.5 and 1.5. `uinv_anc`: upper triangular: zero below the diagonal, diagonal between 0.5 and 1.5. `linv_anc`: lower triangular: zero above the diagonal, diagonal between 0.5 and 1.5. `row_map`: within one replica the entries are distinct. Leaf block row i lies in the k-th of 8 equal ranges of leaf block rows, and its target lies in the k-th of 8 equal ranges of the 64 ancestor block rows. `col_map`: within one replica the entries are distinct. Leaf block column j lies in the k-th of 8 equal ranges of leaf block columns, and its target lies in the k-th of 8 equal ranges of the 64 ancestor block columns.
All inputs are finite; a program needn't handle non-finite values.
Results may differ from a plain program's by a relative error of at most 0.0001.
Values sent between devices are 32-bit elements; how exact they have to be, the bound alone decides.
No kernel may reach another device: no remote copies, remote signals or barrier semaphores. Data moves between devices by JAX's collectives and lax.ppermute only.
A program may use at most 128 MiB of HBM per device.

v0:
```python
import math
import jax
import jax.numpy as jnp
from jax import lax
from jax.sharding import PartitionSpec as P

NB = 128


def in_one_piece(arrays, axis, split_dim, concat_dim, along):
    widths = [math.prod(a.shape[along:]) for a in arrays]
    both = jnp.concatenate(
        [a.reshape(*a.shape[:along], w) for a, w in zip(arrays, widths)], axis=along
    )
    out = lax.all_to_all(both, axis, split_axis=split_dim, concat_axis=concat_dim, tiled=True)
    tiles = jnp.split(out, [sum(widths[:k]) for k in range(1, len(widths))], axis=along)
    return tuple((b.reshape(*out.shape[:along], *a.shape[along:]) for a, b in zip(arrays, tiles)))


def sent_to_all(shard, axis):
    copies = jnp.broadcast_to(shard, (lax.axis_size(axis), *shard.shape))
    return lax.all_to_all(copies, axis, split_axis=0, concat_axis=0, tiled=True)


def in_order(tiles, dim):
    lengths = list(tiles.shape[1:])
    lengths[dim] *= tiles.shape[0]
    return jnp.moveaxis(tiles, 0, dim).reshape(lengths)


def collect(shard, axis, dim):
    tiles = sent_to_all(shard, axis)
    return in_order(tiles, dim)


def gather_axes(shard, axes, dim):
    out = shard
    for number in range(len(axes) - 1, -1, -1):
        out = lax.all_gather(out, axes[number], axis=dim, tiled=True)
    return out


def product(left, right):
    return jnp.dot(left, right, precision=lax.Precision.HIGHEST, preferred_element_type=jnp.float32)


def combine_depth(schur, row_map, col_map, a22_anc):
    block_size = NB
    rows_here = schur.shape[0]
    cols_here = schur.shape[1]
    leaf_rows = rows_here // block_size
    leaf_cols = cols_here // block_size
    anc_rows = a22_anc.shape[0]
    replicas = lax.axis_size("depth")
    anc_row_blocks = anc_rows * replicas // block_size
    anc_col_blocks = a22_anc.shape[1] // block_size
    row_local = row_map[0] - lax.axis_index("row") * anc_row_blocks
    col_local = col_map[0] - lax.axis_index("col") * anc_col_blocks
    owner_blocks = anc_rows // block_size
    slots = min(leaf_rows, owner_blocks)
    owner = row_local // owner_blocks
    earlier = lax.iota(jnp.int32, leaf_rows)[:, None] > lax.iota(jnp.int32, leaf_rows)[None, :]
    same = owner[:, None] == owner[None, :]
    rank = jnp.sum((earlier & same).astype(jnp.int32), axis=1)
    select = (
        (owner[:, None, None] == lax.iota(jnp.int32, replicas)[None, :, None])
        & (rank[:, None, None] == lax.iota(jnp.int32, slots)[None, None, :])
    ).astype(jnp.float32)
    leaf_blocks = schur.reshape(leaf_rows, block_size, cols_here)
    packed = jnp.einsum("iqs,ixc->qsxc", select, leaf_blocks, precision=lax.Precision.HIGHEST)
    packed = packed.reshape(replicas, slots * block_size, cols_here)
    target = (row_local - owner * owner_blocks + 1).astype(jnp.float32)
    tags = jnp.einsum("iqs,i->qs", select, target, precision=lax.Precision.HIGHEST) - 1.0
    col_tags = jnp.broadcast_to(col_local.astype(jnp.float32)[None, :], (replicas, leaf_cols))
    got_rows, got_tags, got_cols = in_one_piece((packed, tags, col_tags), "depth", 0, 0, 1)
    slot_pick = (
        got_tags[:, :, None] == lax.iota(jnp.int32, owner_blocks).astype(jnp.float32)[None, None, :]
    ).astype(jnp.float32)
    column_pick = (
        got_cols[:, :, None]
        == lax.iota(jnp.int32, anc_col_blocks).astype(jnp.float32)[None, None, :]
    ).astype(jnp.float32)
    pieces = got_rows.reshape(replicas, slots, block_size, leaf_cols, block_size)
    sectioned = jnp.einsum("psa,psxjy->paxjy", slot_pick, pieces, precision=lax.Precision.HIGHEST)
    placed = jnp.einsum("paxjy,pjb->axby", sectioned, column_pick, precision=lax.Precision.HIGHEST)
    return placed.reshape(anc_rows, anc_col_blocks * block_size)


def anc_panels(a21_anc, a12_anc, uinv_anc, linv_anc):
    factor = uinv_anc
    anc_lower = product(collect(a21_anc, "col", 1), factor)
    lower_whole = collect(anc_lower, "col", 1)
    factor = linv_anc
    anc_upper = product(factor, lax.all_gather(a12_anc, ("row", "depth"), axis=0, tiled=True))
    return (anc_lower, lower_whole, anc_upper)


def shards(
    a21_leaf,
    a12_leaf,
    uinv_leaf,
    linv_leaf,
    live,
    row_map,
    col_map,
    a22_anc,
    a21_anc,
    a12_anc,
    uinv_anc,
    linv_anc,
):
    block_size = NB
    panel_left = a21_leaf[0]
    panel_top = a12_leaf[0]
    upper_inverse = uinv_leaf[0]
    lower_inverse = linv_leaf[0]
    rows_here = panel_left.shape[0]
    cols_here = panel_top.shape[1]
    live_rows = live[0] * block_size
    row_pos = lax.axis_index("row") * rows_here + lax.iota(jnp.int32, rows_here)
    col_pos = lax.axis_index("col") * cols_here + lax.iota(jnp.int32, cols_here)
    row_keep = (row_pos < live_rows).astype(jnp.float32)
    col_keep = (col_pos < live_rows).astype(jnp.float32)
    factor = upper_inverse
    lower_part = product(lax.all_gather(panel_left, "col", axis=1, tiled=True), factor)
    leaf_lower = lower_part * row_keep[:, None]
    factor = lower_inverse
    upper_part = product(factor, lax.all_gather(panel_top, "row", axis=0, tiled=True))
    leaf_upper = upper_part * col_keep[None, :]
    upper_whole = lax.all_gather(leaf_upper, "row", axis=0, tiled=True)
    factor = upper_whole
    schur = jnp.zeros((rows_here, cols_here), jnp.float32) - product(
        lax.all_gather(leaf_lower, "col", axis=1, tiled=True), factor
    )
    own_update = combine_depth(schur, row_map, col_map, a22_anc)
    anc_lower, lower_whole, anc_upper = anc_panels(a21_anc, a12_anc, uinv_anc, linv_anc)
    factor = lower_whole
    anc_schur = a22_anc + own_update - product(factor, gather_axes(anc_upper, ("row", "depth"), 0))
    return (leaf_lower[None], leaf_upper[None], anc_lower, anc_upper, anc_schur)


def solution(mesh):
    in_specs = (
        P("depth", "row", "col"),
        P("depth", "row", "col"),
        P("depth", None, "col"),
        P("depth", "row", None),
        P("depth"),
        P("depth", "row"),
        P("depth", "col"),
        P(("row", "depth"), "col"),
        P(("row", "depth"), "col"),
        P(("row", "depth"), "col"),
        P(None, "col"),
        P(("row", "depth"), None),
    )
    out_specs = (
        P("depth", "row", "col"),
        P("depth", "row", "col"),
        P(("row", "depth"), "col"),
        P(("row", "depth"), "col"),
        P(("row", "depth"), "col"),
    )
    return jax.shard_map(shards, mesh=mesh, in_specs=in_specs, out_specs=out_specs, check_vma=False)
```

profile of v0, /device:TPU:1, one launch (start us, length us, event | category | flops | bytes accessed | tf_op | source)
XLA Modules:
  0.0 436.7 jit_solution(4254180319421357973)
XLA Ops:
  7.2 0.0 all-gather.20.cloned.1.call-start
  7.2 0.7 all-gather.20.cloned.1.call-update
  7.9 0.0 all-gather.22.cloned.1.call-start
  8.0 0.7 all-gather.22.cloned.1.call-update
  8.7 0.0 all-gather.10.cloned.1.call-start
  8.7 0.7 all-gather.10.cloned.1.call-update
  9.4 0.0 all-gather.12.cloned.1.call-start
  10.1 38.6 %all-gather.20.cloned.1.call-done = f32[1,512,2048]{2,1,0:T(8,128)} async-done(((f32[1,512,256]{2,1,0:T(8,128)}), f32[1,512,2048]{2,1,0:T(8,128)}) %all-gather.20.cloned.1.call-update) | async-done | bytes 4194320 | tf_op jit(solution)/shard_map/all_gather | solution.py:125
  48.7 6.4 %fusion.10 = f32[512,256]{1,0:T(8,128)} fusion(f32[1,2048,256]{2,1,0:T(8,128)S(1)} %copy-done, f32[1,512,2048]{2,1,0:T(8,128)} %all-gather.20.cloned.1.call-done, f32[512]{0:T(512)S(1)} %fusion.32), kind=kOutput, calls=%fused_computation.13 | convolution fusion | flops 3221356544 | bytes 6817792 | tf_op jit(solution)/shard_map/dot_general | solution.py:44
  55.1 0.0 all-gather.12.cloned.1.call-update
  55.1 0.0 all-gather.14.cloned.1.call-start
  55.2 49.4 %all-gather.22.cloned.1.call-done = f32[1,2048,512]{2,1,0:T(8,128)} async-done(((f32[1,256,512]{2,1,0:T(8,128)}), f32[1,2048,512]{2,1,0:T(8,128)}) %all-gather.22.cloned.1.call-update) | async-done | bytes 4194320 | tf_op jit(solution)/shard_map/all_gather | solution.py:128
  104.6 7.3 %fusion.15 = f32[256,512]{1,0:T(8,128)} fusion(f32[1,2048,512]{2,1,0:T(8,128)} %all-gather.22.cloned.1.call-done, f32[1,256,2048]{2,1,0:T(8,128)} %param.15, f32[512]{0:T(512)S(1)} %fusion.33), kind=kOutput, calls=%fused_computation.14 | convolution fusion | flops 3221356544 | bytes 6817792 | tf_op jit(solution)/shard_map/dot_general | solution.py:44
  112.0 0.1 copy.29
  112.1 1.5 broadcast_in_dim.16
  113.6 5.3 %all-to-all-start = ((f32[8,256,256]{1,2,0:T(8,128)}), f32[8,256,256]{1,2,0:T(8,128)S(1)}, u32[]{:S(2)}, u32[]{:S(2)}) async-start(f32[8,256,256]{1,2,0:T(8,128)} %broadcast_in_dim.16), calls=%async_computation | async-start | bytes 4194304 | tf_op jit(solution)/shard_map/all_to_all | solution.py:22
  118.9 0.1 convert_reduce_fusion
  119.0 84.1 %all-gather.10.cloned.1.call-done = f32[2048,1024]{1,0:T(8,128)} async-done(((f32[64,1024]{1,0:T(8,128)}), f32[2048,1024]{1,0:T(8,128)}) %all-gather.10.cloned.1.call-update) | async-done | bytes 8388624 | tf_op jit(solution)/shard_map/all_gather | solution.py:94
  203.1 8.2 %fusion.51 = f32[64,1024]{1,0:T(8,128)} fusion(f32[64,2048]{1,0:T(8,128)S(1)} %copy-done.3, f32[2048,1024]{1,0:T(8,128)} %all-gather.10.cloned.1.call-done), kind=kOutput, calls=%fused_computation.69 | convolution fusion | flops 1610612736 | bytes 9175040 | tf_op jit(solution)/shard_map/dot_general | solution.py:44
  211.4 0.2 all-gather.18.cloned.1.call-start
  211.6 0.1 fusion.27
  211.7 0.1 copy.37
  211.8 0.1 bitcast_add_fusion.1
  211.9 26.4 %all-gather.12.cloned.1.call-done = f32[512,2048]{1,0:T(8,128)} async-done(((f32[512,256]{1,0:T(8,128)}), f32[512,2048]{1,0:T(8,128)}) %all-gather.12.cloned.1.call-update) | async-done | bytes 4194320 | tf_op jit(solution)/shard_map/all_gather | solution.py:133
  238.3 56.4 %all-gather.14.cloned.1.call-done = f32[2048,512]{1,0:T(8,128)} async-done(((f32[256,512]{1,0:T(8,128)}), f32[2048,512]{1,0:T(8,128)}) %all-gather.14.cloned.1.call-update) | async-done | bytes 4194320 | tf_op jit(solution)/shard_map/all_gather | solution.py:130
  294.7 9.4 %convolution_subtract_fusion = f32[512,512]{1,0:T(8,128)S(1)} fusion(f32[512,2048]{1,0:T(8,128)} %all-gather.12.cloned.1.call-done, f32[2048,512]{1,0:T(8,128)} %all-gather.14.cloned.1.call-done), kind=kOutput, calls=%fused_computation.11 | convolution fusion | flops 6442713088 | bytes 9437184 | tf_op jit(solution)/shard_map/dot_general | solution.py:44
  304.0 3.6 fusion.20
  307.6 12.7 %all-gather.16.cloned.1.call-done = f32[256,1024]{1,0:T(8,128)} async-done(((f32[64,1024]{1,0:T(8,128)}), f32[256,1024]{1,0:T(8,128)}) %all-gather.16.cloned.1.call-update) | async-done | bytes 1048592 | tf_op jit(solution)/shard_map/all_gather | solution.py:39
  320.3 3.1 constant_dynamic-update-slice_fusion
  323.4 1.3 dynamic-update-slice.1
  324.7 1.4 dynamic-update-slice.2
  326.0 4.8 %copy.31 = f32[4,1,131078]{2,1,0:T(1,128)} copy(f32[4,1,131078]{2,0,1:T(4,128)} %bitcast.99) | data formatting | bytes 4194496 | tf_op jit(solution)/shard_map/all_to_all | solution.py:15
  330.9 4.5 %all-to-all-start.1 = ((f32[4,1,131078]{2,1,0:T(1,128)}), f32[4,1,131078]{2,1,0:T(1,128)}, u32[]{:S(2)}, u32[]{:S(2)}) async-start(f32[4,1,131078]{2,1,0:T(1,128)} %copy.31), calls=%async_computation.1 | async-start | bytes 4198400 | tf_op jit(solution)/shard_map/all_to_all | solution.py:15
  335.4 5.3 %fusion.50 = f32[256,256]{1,0:T(8,128)S(1)} fusion(f32[256,2048]{0,1:T(8,128)S(1)} %bitcast.100, f32[2048,256]{1,0:T(8,128)} %param.22), kind=kOutput, calls=%fused_computation.68 | convolution fusion | flops 1610612736 | bytes 4456448 | tf_op jit(solution)/shard_map/dot_general | solution.py:44
  340.7 0.1 copy.35
  340.8 18.3 %all-to-all-done.1 = f32[4,1,131078]{2,1,0:T(1,128)} async-done(((f32[4,1,131078]{2,1,0:T(1,128)}), f32[4,1,131078]{2,1,0:T(1,128)}, u32[]{:S(2)}, u32[]{:S(2)}) %all-to-all-start.1) | async-done | bytes 2097280 | tf_op jit(solution)/shard_map/all_to_all | solution.py:15
  359.1 1.5 broadcast_in_dim.20
  360.6 7.9 %all-to-all-start.2 = ((f32[8,256,256]{1,2,0:T(8,128)}), f32[8,256,256]{1,2,0:T(8,128)}, u32[]{:S(2)}, u32[]{:S(2)}) async-start(f32[8,256,256]{1,2,0:T(8,128)} %broadcast_in_dim.20), calls=%async_computation.2 | async-start | bytes 4194304 | tf_op jit(solution)/shard_map/all_to_all | solution.py:22
  368.5 2.6 copy.53
  371.2 1.5 split.14
  372.7 0.1 split.12
  372.8 3.4 reshape_reshape.7
  376.2 0.1 copy.32
  376.2 4.8 %fusion.8 = f32[4,2,128,4,128]{4,1,3,2,0:T(2,128)S(1)} fusion(f32[4,2,128,4,128]{4,3,2,1,0:T(4,128)S(1)} %reshape_reshape.7, f32[4,2]{1,0:T(4,128)S(1)} %split.13, f32[2]{0:T(128)S(1)} %iota_convert_fusion), kind=kOutput, calls=%fused_computation.9 | convolution fusion | flops 12582928 | bytes 4194344 | tf_op jit(solution)/shard_map/psa,psxjy->paxjy/dot_general | solution.py:84
  381.0 3.2 fusion.6
  384.3 10.6 %all-to-all-done.2 = f32[8,256,256]{1,2,0:T(8,128)} async-done(((f32[8,256,256]{1,2,0:T(8,128)}), f32[8,256,256]{1,2,0:T(8,128)}, u32[]{:S(2)}, u32[]{:S(2)}) %all-to-all-start.2) | async-done | bytes 2097184 | tf_op jit(solution)/shard_map/all_to_all | solution.py:22
  394.8 23.6 %all-gather.18.cloned.1.call-done = f32[2048,1024]{1,0:T(8,128)} async-done(((f32[256,1024]{1,0:T(8,128)}), f32[2048,1024]{1,0:T(8,128)}) %all-gather.18.cloned.1.call-update) | async-done | bytes 8388624 | tf_op jit(solution)/shard_map/all_gather | solution.py:39
  418.5 11.4 %convolution_subtract_fusion.1 = f32[256,1024]{1,0:T(8,128)} fusion(f32[256,2048]{0,1:T(8,128)} %bitcast.28, f32[2048,1024]{1,0:T(8,128)} %all-gather.18.cloned.1.call-done, f32[256,1024]{1,0:T(8,128)} %param.19, f32[32,8,8,128]{3,2,1,0:T(8,128)S(1)} %bitcast.103), kind=kOutput, calls=%fused_computation.12 | convolution fusion | flops 6442975232 | bytes 13631488 | tf_op jit(solution)/shard_map/dot_general | solution.py:44
  (30 shorter events, 0.2 us)
Async XLA Ops:
  7.2 41.5 %copy-start = (f32[1,2048,256]{2,1,0:T(8,128)S(1)}, f32[1,2048,256]{2,1,0:T(8,128)}, u32[]{:S(2)}) copy-start(f32[1,2048,256]{2,1,0:T(8,128)} %param.14) | copy-start | bytes 6291460
  7.2 41.5 %all-gather.20.cloned.1.call-start = ((), (), s32[]{:S(2)}) async-start(), calls=%async_computation.8 | async-start | bytes 4718592 | tf_op jit(solution)/shard_map/all_gather | solution.py:125
  7.9 96.7 %all-gather.22.cloned.1.call-start = ((), (), s32[]{:S(2)}) async-start(), calls=%async_computation.9 | async-start | bytes 4718592 | tf_op jit(solution)/shard_map/all_gather | solution.py:128
  8.7 194.5 %all-gather.10.cloned.1.call-start = ((), (), s32[]{:S(2)}) async-start(), calls=%async_computation.3 | async-start | bytes 8650752 | tf_op jit(solution)/shard_map/all_gather | solution.py:94
  9.4 228.9 %all-gather.12.cloned.1.call-start = ((), (), s32[]{:S(2)}) async-start(), calls=%async_computation.4 | async-start | bytes 4718592 | tf_op jit(solution)/shard_map/all_gather | solution.py:133
  55.1 239.5 %all-gather.14.cloned.1.call-start = ((), (), s32[]{:S(2)}) async-start(), calls=%async_computation.5 | async-start | bytes 4718592 | tf_op jit(solution)/shard_map/all_gather | solution.py:130
  55.2 56.8 %copy-start.4 = (f32[256,256]{1,0:T(8,128)S(1)}, f32[256,256]{1,0:T(8,128)}, u32[]{:S(2)}) copy-start(f32[256,256]{1,0:T(8,128)} %param.20) | copy-start | bytes 786436
  113.6 5.3 %copy-start.5 = (s32[1,4]{1,0:T(1,128)S(1)}, s32[1,4]{1,0:T(1,128)}, u32[]{:S(2)}) copy-start(s32[1,4]{1,0:T(1,128)} %param.17) | copy-start | bytes 52
  113.6 89.5 %copy-start.3 = (f32[64,2048]{1,0:T(8,128)S(1)}, f32[64,2048]{1,0:T(8,128)}, u32[]{:S(2)}) copy-start(f32[64,2048]{1,0:T(8,128)} %param.23) | copy-start | bytes 1572868
  113.6 217.2 %all-to-all-start = ((f32[8,256,256]{1,2,0:T(8,128)}), f32[8,256,256]{1,2,0:T(8,128)S(1)}, u32[]{:S(2)}, u32[]{:S(2)}) async-start(f32[8,256,256]{1,2,0:T(8,128)} %broadcast_in_dim.16), calls=%async_computation | async-start | bytes 4194304 | tf_op jit(solution)/shard_map/all_to_all | solution.py:22
  118.9 201.4 %all-gather.16.cloned.1.call-start = ((), (), s32[]{:S(2)}) async-start(), calls=%async_computation.6 | async-start | bytes 1310720 | tf_op jit(solution)/shard_map/all_gather | solution.py:39
  119.0 92.8 %copy-start.6 = (s32[1,4]{1,0:T(1,128)S(1)}, s32[1,4]{1,0:T(1,128)}, u32[]{:S(2)}) copy-start(s32[1,4]{1,0:T(1,128)} %param.18) | copy-start | bytes 52
  211.4 207.1 %all-gather.18.cloned.1.call-start = ((), (), s32[]{:S(2)}) async-start(), calls=%async_computation.7 | async-start | bytes 9437184 | tf_op jit(solution)/shard_map/all_gather | solution.py:39
  330.9 28.3 %all-to-all-start.1 = ((f32[4,1,131078]{2,1,0:T(1,128)}), f32[4,1,131078]{2,1,0:T(1,128)}, u32[]{:S(2)}, u32[]{:S(2)}) async-start(f32[4,1,131078]{2,1,0:T(1,128)} %copy.31), calls=%async_computation.1 | async-start | bytes 4198400 | tf_op jit(solution)/shard_map/all_to_all | solution.py:15
  340.7 20.0 %copy-start.2 = (f32[256,256]{1,0:T(8,128)}, f32[256,256]{1,0:T(8,128)S(1)}, u32[]{:S(2)}) copy-start(f32[256,256]{1,0:T(8,128)S(1)} %fusion.50) | copy-start | bytes 786436
  360.6 34.2 %all-to-all-start.2 = ((f32[8,256,256]{1,2,0:T(8,128)}), f32[8,256,256]{1,2,0:T(8,128)}, u32[]{:S(2)}, u32[]{:S(2)}) async-start(f32[8,256,256]{1,2,0:T(8,128)} %broadcast_in_dim.20), calls=%async_computation.2 | async-start | bytes 4194304 | tf_op jit(solution)/shard_map/all_to_all | solution.py:22
  418.5 11.4 %copy-start.1 = (f32[1,2048,256]{2,1,0:T(8,128)S(1)}, f32[1,2048,256]{2,1,0:T(8,128)}, u32[]{:S(2)}) copy-start(f32[1,2048,256]{2,1,0:T(8,128)} %param.14) | copy-start | bytes 6291460
Sparse Core Ops, SparseCore 0:
  9.8 38.8 all-gather.19
  50.5 54.1 all-gather.21
  107.2 95.8 all-gather.9
  205.4 32.8 all-gather.11
  240.5 54.1 all-gather.13
  296.9 23.3 all-gather.15
  322.0 96.3 all-gather.17
where the time goes:
time: 437 us
  waiting for transfers between devices  322 us (74%)
  matrix products  59.7 us (14%)
  local copies, waits for them, and re-layouts  21.7 us (5%)
  starting transfers between devices  18.1 us (4%)
  between operations  14.9 us (3%)
    all_gather x1, waiting for transfers between devices, anc_panels(): lax.all_gather(a12_anc, ('row', 'depth'), axis=0, tiled=True)  84.1 us
    all_gather x1, waiting for transfers between devices, shards(): upper_whole = lax.all_gather(leaf_upper, 'row', axis=0, tiled=True)  56.4 us
    all_gather x1, waiting for transfers between devices, shards(): lax.all_gather(panel_top, 'row', axis=0, tiled=True)  49.4 us
    dot_general x6, matrix products, product(): jnp.dot(left, right, precision=lax.Precision.HIGHEST, preferred_element_t...  48 us
    all_gather x1, waiting for transfers between devices, shards(): lax.all_gather(panel_left, 'col', axis=1, tiled=True)  38.6 us
    all_gather x2, waiting for transfers between devices, gather_axes(): out = lax.all_gather(out, axes[number], axis=dim, tiled=True)  36.3 us
    all_gather x1, waiting for transfers between devices, shards(): lax.all_gather(leaf_lower, 'col', axis=1, tiled=True)  26.4 us
    all_to_all x1, waiting for transfers between devices, in_one_piece(): lax.all_to_all(both, axis, split_axis=split_dim, concat_axis=concat_dim,...  18.3 us
  transfers between devices with their start and end apart: 10, of which 9 were waited for; matrix products, arithmetic and copies ran while one was open for 16% of the time, Pallas kernels for 0%

commit v1 on v0

--- a/solution.py
+++ b/solution.py
@@ -125,7 +125,12 @@
     lower_part = product(lax.all_gather(panel_left, "col", axis=1, tiled=True), factor)
     leaf_lower = lower_part * row_keep[:, None]
     factor = lower_inverse
-    upper_part = product(factor, lax.all_gather(panel_top, "row", axis=0, tiled=True))
+    upper_part = product(
+        factor,
+        jnp.concatenate(
+            lax.all_to_all(jnp.stack([panel_top] * lax.axis_size("row")), "row", 0, 0), axis=0
+        ),
+    )
     leaf_upper = upper_part * col_keep[None, :]
     upper_whole = lax.all_gather(leaf_upper, "row", axis=0, tiled=True)
     factor = upper_whole

time: 437 us -> 416 us (0.952)
  waiting for transfers between devices: 322 us -> 288 us
  starting transfers between devices: 18.1 us -> 26.9 us
    all_to_all x0 -> x1, waiting for transfers between devices: none -> 106 us  [shards(): lax.all_to_all(jnp.stack([panel_top] * lax.axis_size('row')), 'row', 0, 0)]
    all_gather x1, waiting for transfers between devices: 84.1 us -> 32.7 us  [anc_panels(): lax.all_gather(a12_anc, ('row', 'depth'), axis=0, tiled=True)]
    all_gather x1 -> x0, waiting for transfers between devices: 49.4 us -> none  [shards(): lax.all_gather(panel_top, 'row', axis=0, tiled=True)]
    all_gather x1, waiting for transfers between devices: 38.6 us -> 0.02 us  [shards(): lax.all_gather(panel_left, 'col', axis=1, tiled=True)]
    all_gather x1, waiting for transfers between devices: 56.4 us -> 46.1 us  [shards(): upper_whole = lax.all_gather(leaf_upper, 'row', axis=0, tiled=True)]
    all_gather x1, waiting for transfers between devices: 26.4 us -> 36.1 us  [shards(): lax.all_gather(leaf_lower, 'col', axis=1, tiled=True)]
    all_to_all x0 -> x1, starting transfers between devices: none -> 9 us  [shards(): lax.all_to_all(jnp.stack([panel_top] * lax.axis_size('row')), 'row', 0, 0)]
  transfers between devices with their start and end apart: 10 -> 10, of which waited for: 9 -> 8; matrix products, arithmetic and copies ran while one was open for 16% -> 18% of each run, Pallas kernels for 0% -> 0%
where the time goes in v1:
time: 416 us
  waiting for transfers between devices  288 us (69%)
  matrix products  60.3 us (14%)
  starting transfers between devices  26.9 us (6%)
  local copies, waits for them, and re-layouts  25 us (6%)
  between operations  14.9 us (4%)
    all_to_all x1, waiting for transfers between devices, shards(): lax.all_to_all(jnp.stack([panel_top] * lax.axis_size('row')), 'row', 0, 0)  106 us
    dot_general x6, matrix products, product(): jnp.dot(left, right, precision=lax.Precision.HIGHEST, preferred_element_t...  48.6 us
    all_gather x1, waiting for transfers between devices, shards(): upper_whole = lax.all_gather(leaf_upper, 'row', axis=0, tiled=True)  46.1 us
    all_gather x2, waiting for transfers between devices, gather_axes(): out = lax.all_gather(out, axes[number], axis=dim, tiled=True)  37.1 us
    all_gather x1, waiting for transfers between devices, shards(): lax.all_gather(leaf_lower, 'col', axis=1, tiled=True)  36.1 us
    all_gather x1, waiting for transfers between devices, anc_panels(): lax.all_gather(a12_anc, ('row', 'depth'), axis=0, tiled=True)  32.7 us
    all_to_all x1, waiting for transfers between devices, in_one_piece(): lax.all_to_all(both, axis, split_axis=split_dim, concat_axis=concat_dim,...  18.3 us
    all_to_all x2, starting transfers between devices, sent_to_all(): return lax.all_to_all(copies, axis, split_axis=0, concat_axis=0, tiled=True)  13 us
  transfers between devices with their start and end apart: 10, of which 8 were waited for; matrix products, arithmetic and copies ran while one was open for 18% of the time, Pallas kernels for 0%

profile of v1, /device:TPU:1, one launch (start us, length us, event | category | flops | bytes accessed | tf_op | source)
XLA Modules:
  0.0 415.6 jit_solution(11740447970734659301)
XLA Ops:
  7.2 0.0 all-gather.18.cloned.1.call-start
  7.2 0.7 all-gather.18.cloned.1.call-update
  7.9 0.0 all-gather.8.cloned.1.call-start
  8.0 0.7 all-gather.8.cloned.1.call-update
  8.7 3.5 stack.3
  12.2 9.0 %all-to-all-start = ((f32[8,256,512]{2,1,0:T(8,128)}), f32[8,256,512]{2,1,0:T(8,128)}, u32[]{:S(2)}, u32[]{:S(2)}) async-start(f32[8,256,512]{2,1,0:T(8,128)} %stack.3), calls=%async_computation | async-start | bytes 8388608 | tf_op jit(solution)/shard_map/all_to_all | solution.py:131
  21.2 0.0 all-gather.12.cloned.1.call-start
  21.9 106.0 %all-to-all-done = f32[8,256,512]{2,1,0:T(8,128)} async-done(((f32[8,256,512]{2,1,0:T(8,128)}), f32[8,256,512]{2,1,0:T(8,128)}, u32[]{:S(2)}, u32[]{:S(2)}) %all-to-all-start) | async-done | bytes 4194336 | tf_op jit(solution)/shard_map/all_to_all | solution.py:131
  127.9 6.7 %fusion.9 = f32[256,512]{1,0:T(8,128)} fusion(f32[2048,512]{1,0:T(8,128)} %bitcast.6, f32[1,256,2048]{2,1,0:T(8,128)S(1)} %copy-done, f32[512]{0:T(512)S(1)} %fusion.30), kind=kOutput, calls=%fused_computation.12 | convolution fusion | flops 3221356544 | bytes 6817792 | tf_op jit(solution)/shard_map/dot_general | solution.py:44
  134.6 0.0 all-gather.12.cloned.1.call-update
  134.6 0.0 all-gather.10.cloned.1.call-start
  134.7 0.0 all-gather.18.cloned.1.call-done
  134.7 7.7 %fusion.12 = f32[512,256]{1,0:T(8,128)} fusion(f32[1,2048,256]{2,1,0:T(8,128)} %param.14, f32[1,512,2048]{2,1,0:T(8,128)} %all-gather.18.cloned.1.call-done, f32[512]{0:T(512)S(1)} %fusion.29), kind=kOutput, calls=%fused_computation.13 | convolution fusion | flops 3221356544 | bytes 6817792 | tf_op jit(solution)/shard_map/dot_general | solution.py:44
  142.4 0.1 copy.29
  142.5 1.5 broadcast_in_dim.16
  144.0 5.1 %all-to-all-start.1 = ((f32[8,256,256]{1,2,0:T(8,128)}), f32[8,256,256]{1,2,0:T(8,128)S(1)}, u32[]{:S(2)}, u32[]{:S(2)}) async-start(f32[8,256,256]{1,2,0:T(8,128)} %broadcast_in_dim.16), calls=%async_computation.1 | async-start | bytes 4194304 | tf_op jit(solution)/shard_map/all_to_all | solution.py:22
  149.2 0.1 convert_reduce_fusion
  149.3 32.7 %all-gather.8.cloned.1.call-done = f32[2048,1024]{1,0:T(8,128)} async-done(((f32[64,1024]{1,0:T(8,128)}), f32[2048,1024]{1,0:T(8,128)}) %all-gather.8.cloned.1.call-update) | async-done | bytes 8388624 | tf_op jit(solution)/shard_map/all_gather | solution.py:94
  181.9 8.2 %fusion.48 = f32[64,1024]{1,0:T(8,128)} fusion(f32[64,2048]{1,0:T(8,128)S(1)} %copy-done.3, f32[2048,1024]{1,0:T(8,128)} %all-gather.8.cloned.1.call-done), kind=kOutput, calls=%fused_computation.68 | convolution fusion | flops 1610612736 | bytes 9175040 | tf_op jit(solution)/shard_map/dot_general | solution.py:44
  190.2 0.2 all-gather.16.cloned.1.call-start
  190.4 0.1 fusion.24
  190.5 0.1 copy.37
  190.6 0.1 bitcast_add_fusion.1
  190.7 46.1 %all-gather.12.cloned.1.call-done = f32[2048,512]{1,0:T(8,128)} async-done(((f32[256,512]{1,0:T(8,128)}), f32[2048,512]{1,0:T(8,128)}) %all-gather.12.cloned.1.call-update) | async-done | bytes 4194320 | tf_op jit(solution)/shard_map/all_gather | solution.py:135
  236.8 36.1 %all-gather.10.cloned.1.call-done = f32[512,2048]{1,0:T(8,128)} async-done(((f32[512,256]{1,0:T(8,128)}), f32[512,2048]{1,0:T(8,128)}) %all-gather.10.cloned.1.call-update) | async-done | bytes 4194320 | tf_op jit(solution)/shard_map/all_gather | solution.py:138
  272.9 9.3 %convolution_subtract_fusion = f32[512,512]{1,0:T(8,128)S(1)} fusion(f32[512,2048]{1,0:T(8,128)} %all-gather.10.cloned.1.call-done, f32[2048,512]{1,0:T(8,128)} %all-gather.12.cloned.1.call-done), kind=kOutput, calls=%fused_computation.10 | convolution fusion | flops 6442713088 | bytes 9437184 | tf_op jit(solution)/shard_map/dot_general | solution.py:44
  282.2 3.6 fusion.17
  285.8 13.5 %all-gather.14.cloned.1.call-done = f32[256,1024]{1,0:T(8,128)} async-done(((f32[64,1024]{1,0:T(8,128)}), f32[256,1024]{1,0:T(8,128)}) %all-gather.14.cloned.1.call-update) | async-done | bytes 1048592 | tf_op jit(solution)/shard_map/all_gather | solution.py:39
  299.2 3.1 constant_dynamic-update-slice_fusion
  302.4 1.2 dynamic-update-slice.1
  303.5 1.3 dynamic-update-slice.2
  304.8 4.8 %copy.31 = f32[4,1,131078]{2,1,0:T(1,128)} copy(f32[4,1,131078]{2,0,1:T(4,128)} %bitcast.97) | data formatting | bytes 4194496 | tf_op jit(solution)/shard_map/all_to_all | solution.py:15
  309.6 4.5 %all-to-all-start.2 = ((f32[4,1,131078]{2,1,0:T(1,128)}), f32[4,1,131078]{2,1,0:T(1,128)}, u32[]{:S(2)}, u32[]{:S(2)}) async-start(f32[4,1,131078]{2,1,0:T(1,128)} %copy.31), calls=%async_computation.2 | async-start | bytes 4198400 | tf_op jit(solution)/shard_map/all_to_all | solution.py:15
  314.2 5.3 %fusion.47 = f32[256,256]{1,0:T(8,128)S(1)} fusion(f32[256,2048]{0,1:T(8,128)S(1)} %bitcast.98, f32[2048,256]{1,0:T(8,128)} %param.22), kind=kOutput, calls=%fused_computation.67 | convolution fusion | flops 1610612736 | bytes 4456448 | tf_op jit(solution)/shard_map/dot_general | solution.py:44
  319.5 0.1 copy.35
  319.6 18.3 %all-to-all-done.2 = f32[4,1,131078]{2,1,0:T(1,128)} async-done(((f32[4,1,131078]{2,1,0:T(1,128)}), f32[4,1,131078]{2,1,0:T(1,128)}, u32[]{:S(2)}, u32[]{:S(2)}) %all-to-all-start.2) | async-done | bytes 2097280 | tf_op jit(solution)/shard_map/all_to_all | solution.py:15
  337.9 1.5 broadcast_in_dim.20
  339.4 7.9 %all-to-all-start.3 = ((f32[8,256,256]{1,2,0:T(8,128)}), f32[8,256,256]{1,2,0:T(8,128)}, u32[]{:S(2)}, u32[]{:S(2)}) async-start(f32[8,256,256]{1,2,0:T(8,128)} %broadcast_in_dim.20), calls=%async_computation.3 | async-start | bytes 4194304 | tf_op jit(solution)/shard_map/all_to_all | solution.py:22
  347.3 2.6 copy.53
  350.0 1.5 split.14
  351.5 0.1 split.12
  351.6 3.4 reshape_reshape.7
  354.9 0.1 copy.32
  355.0 4.8 %fusion.7 = f32[4,2,128,4,128]{4,1,3,2,0:T(2,128)S(1)} fusion(f32[4,2,128,4,128]{4,3,2,1,0:T(4,128)S(1)} %reshape_reshape.7, f32[4,2]{1,0:T(4,128)S(1)} %split.13, f32[2]{0:T(128)S(1)} %iota_convert_fusion), kind=kOutput, calls=%fused_computation.8 | convolution fusion | flops 12582928 | bytes 4194344 | tf_op jit(solution)/shard_map/psa,psxjy->paxjy/dot_general | solution.py:84
  359.8 3.2 fusion.5
  363.0 10.6 %all-to-all-done.3 = f32[8,256,256]{1,2,0:T(8,128)} async-done(((f32[8,256,256]{1,2,0:T(8,128)}), f32[8,256,256]{1,2,0:T(8,128)}, u32[]{:S(2)}, u32[]{:S(2)}) %all-to-all-start.3) | async-done | bytes 2097184 | tf_op jit(solution)/shard_map/all_to_all | solution.py:22
  373.6 23.7 %all-gather.16.cloned.1.call-done = f32[2048,1024]{1,0:T(8,128)} async-done(((f32[256,1024]{1,0:T(8,128)}), f32[2048,1024]{1,0:T(8,128)}) %all-gather.16.cloned.1.call-update) | async-done | bytes 8388624 | tf_op jit(solution)/shard_map/all_gather | solution.py:39
  397.3 11.4 %convolution_subtract_fusion.1 = f32[256,1024]{1,0:T(8,128)} fusion(f32[256,2048]{0,1:T(8,128)} %bitcast.29, f32[2048,1024]{1,0:T(8,128)} %all-gather.16.cloned.1.call-done, f32[256,1024]{1,0:T(8,128)} %param.19, f32[32,8,8,128]{3,2,1,0:T(8,128)S(1)} %bitcast.101), kind=kOutput, calls=%fused_computation.11 | convolution fusion | flops 6442975232 | bytes 13631488 | tf_op jit(solution)/shard_map/dot_general | solution.py:44
  (30 shorter events, 0.2 us)
Async XLA Ops:
  7.2 120.7 %copy-start = (f32[1,256,2048]{2,1,0:T(8,128)S(1)}, f32[1,256,2048]{2,1,0:T(8,128)}, u32[]{:S(2)}) copy-start(f32[1,256,2048]{2,1,0:T(8,128)} %param.15) | copy-start | bytes 6291460
  7.2 127.5 %all-gather.18.cloned.1.call-start = ((), (), s32[]{:S(2)}) async-start(), calls=%async_computation.9 | async-start | bytes 4718592 | tf_op jit(solution)/shard_map/all_gather | solution.py:125
  7.9 174.0 %all-gather.8.cloned.1.call-start = ((), (), s32[]{:S(2)}) async-start(), calls=%async_computation.4 | async-start | bytes 8650752 | tf_op jit(solution)/shard_map/all_gather | solution.py:94
  12.2 115.7 %all-to-all-start = ((f32[8,256,512]{2,1,0:T(8,128)}), f32[8,256,512]{2,1,0:T(8,128)}, u32[]{:S(2)}, u32[]{:S(2)}) async-start(f32[8,256,512]{2,1,0:T(8,128)} %stack.3), calls=%async_computation | async-start | bytes 8388608 | tf_op jit(solution)/shard_map/all_to_all | solution.py:131
  21.2 215.6 %all-gather.12.cloned.1.call-start = ((), (), s32[]{:S(2)}) async-start(), calls=%async_computation.6 | async-start | bytes 4718592 | tf_op jit(solution)/shard_map/all_gather | solution.py:135
  134.6 138.3 %all-gather.10.cloned.1.call-start = ((), (), s32[]{:S(2)}) async-start(), calls=%async_computation.5 | async-start | bytes 4718592 | tf_op jit(solution)/shard_map/all_gather | solution.py:138
  134.6 7.7 %copy-start.4 = (f32[256,256]{1,0:T(8,128)S(1)}, f32[256,256]{1,0:T(8,128)}, u32[]{:S(2)}) copy-start(f32[256,256]{1,0:T(8,128)} %param.20) | copy-start | bytes 786436
  144.0 5.1 %copy-start.5 = (s32[1,4]{1,0:T(1,128)S(1)}, s32[1,4]{1,0:T(1,128)}, u32[]{:S(2)}) copy-start(s32[1,4]{1,0:T(1,128)} %param.17) | copy-start | bytes 52
  144.0 37.9 %copy-start.3 = (f32[64,2048]{1,0:T(8,128)S(1)}, f32[64,2048]{1,0:T(8,128)}, u32[]{:S(2)}) copy-start(f32[64,2048]{1,0:T(8,128)} %param.23) | copy-start | bytes 1572868
  144.0 165.6 %all-to-all-start.1 = ((f32[8,256,256]{1,2,0:T(8,128)}), f32[8,256,256]{1,2,0:T(8,128)S(1)}, u32[]{:S(2)}, u32[]{:S(2)}) async-start(f32[8,256,256]{1,2,0:T(8,128)} %broadcast_in_dim.16), calls=%async_computation.1 | async-start | bytes 4194304 | tf_op jit(solution)/shard_map/all_to_all | solution.py:22
  149.1 150.1 %all-gather.14.cloned.1.call-start = ((), (), s32[]{:S(2)}) async-start(), calls=%async_computation.7 | async-start | bytes 1310720 | tf_op jit(solution)/shard_map/all_gather | solution.py:39
  149.2 41.4 %copy-start.6 = (s32[1,4]{1,0:T(1,128)S(1)}, s32[1,4]{1,0:T(1,128)}, u32[]{:S(2)}) copy-start(s32[1,4]{1,0:T(1,128)} %param.18) | copy-start | bytes 52
  190.2 207.1 %all-gather.16.cloned.1.call-start = ((), (), s32[]{:S(2)}) async-start(), calls=%async_computation.8 | async-start | bytes 9437184 | tf_op jit(solution)/shard_map/all_gather | solution.py:39
  309.6 28.3 %all-to-all-start.2 = ((f32[4,1,131078]{2,1,0:T(1,128)}), f32[4,1,131078]{2,1,0:T(1,128)}, u32[]{:S(2)}, u32[]{:S(2)}) async-start(f32[4,1,131078]{2,1,0:T(1,128)} %copy.31), calls=%async_computation.2 | async-start | bytes 4198400 | tf_op jit(solution)/shard_map/all_to_all | solution.py:15
  319.5 20.0 %copy-start.2 = (f32[256,256]{1,0:T(8,128)}, f32[256,256]{1,0:T(8,128)S(1)}, u32[]{:S(2)}) copy-start(f32[256,256]{1,0:T(8,128)S(1)} %fusion.47) | copy-start | bytes 786436
  339.4 34.2 %all-to-all-start.3 = ((f32[8,256,256]{1,2,0:T(8,128)}), f32[8,256,256]{1,2,0:T(8,128)}, u32[]{:S(2)}, u32[]{:S(2)}) async-start(f32[8,256,256]{1,2,0:T(8,128)} %broadcast_in_dim.20), calls=%async_computation.3 | async-start | bytes 4194304 | tf_op jit(solution)/shard_map/all_to_all | solution.py:22
  397.3 11.4 %copy-start.1 = (f32[1,256,2048]{2,1,0:T(8,128)S(1)}, f32[1,256,2048]{2,1,0:T(8,128)}, u32[]{:S(2)}) copy-start(f32[1,256,2048]{2,1,0:T(8,128)} %param.15) | copy-start | bytes 6291460
Sparse Core Ops, SparseCore 0:
  9.8 38.8 all-gather.17
  51.3 130.6 all-gather.7
  184.3 52.4 all-gather.11
  239.0 33.7 all-gather.9
  275.1 24.0 all-gather.13
  300.9 96.3 all-gather.15
